TPU v7x, 32 devices: a whole 2x2x4 slice. The times are simulated.
32 devices in a mesh: dp: 2 (over x), expert: 4 (over z), mp: 4 (over y, core).
Axes of the slice: x: 2, y: 2, z: 4, core: 2. Of those that a mesh axis runs over, the one named last changes fastest.
Arguments:
- tokens: bfloat16 [512, 4096], P('dp', ('expert', 'mp')), may hold values from -6 to 6
- expert_index: int32 [512, 2], P('dp'), may hold values from 0 to 3, as said below
- slot_index: int32 [512, 2], P('dp'), may hold values from 0 to 191, as said below
- norm_gain: float32 [4096], P(('expert', 'mp')), may hold values from 0.1 to 1.9
- router_weight: bfloat16 [4, 4096], P(None, ('expert', 'mp')), may hold values from -8 to 8
- gate_weight: bfloat16 [4, 7168, 4096], P('expert', ('dp', 'mp')), may hold values from -0.09375 to 0.09375
- up_weight: bfloat16 [4, 7168, 4096], P('expert', ('dp', 'mp')), may hold values from -0.09375 to 0.09375
- down_weight: bfloat16 [4, 7168, 4096], P('expert', ('dp', 'mp')), may hold values from -0.09375 to 0.09375
- final_gain: float32 [4096], replicated, may hold values from 0.1 to 1.9
- head_weight: bfloat16 [16384, 4096], P(('expert', 'mp')), may hold values from -8 to 8
Outputs:
- layer_out: bfloat16 [512, 4096], P('dp', ('expert', 'mp'))
- head_logsum: float32 [512], P('dp')
- router_penalty: float32 [], replicated
- head_penalty: float32 [], replicated
Inputs may be any that keep to these rules, and one draw needn't show every extreme that they name: `expert_index`: each row names 2 different experts. In each aligned block of 256 rows every expert is named at least once and at most 192 times; in every block two experts are named exactly 192 times, and one of them is the same expert in all blocks. `slot_index`: within each aligned block of 256 rows, the choices that name one expert hold the slots 0, 1, 2, ... in the order of rows, and within a row in the order of choices.
All inputs are finite; a program needn't handle non-finite values.
Results may differ from a plain program's by a relative error of at most 0.01115.
Values may be sent and summed in bfloat16 or wider, within the bound.
A program may use at most 128 MiB of HBM per device.

v0:
```python
import jax
import jax.numpy as jnp
from jax import lax
from jax.sharding import PartitionSpec as P

epsilon = 1e-05


def merged(value, axis, join):
    pieces = jax.tree.map(lambda part: lax.all_gather(part, axis), value)
    head = jax.tree.map(lambda part: part[0], pieces)
    tail = jax.tree.map(lambda part: part[1:], pieces)
    running, _ = lax.scan(lambda running, piece: (join(running, piece), None), head, tail)
    return running


def merge_softmax(first_pair, second_pair):
    larger = jnp.maximum(first_pair[0], second_pair[0])
    total = first_pair[1] * jnp.exp(first_pair[0] - larger) + second_pair[1] * jnp.exp(
        second_pair[0] - larger
    )
    return (larger, total)


def body(
    tokens,
    expert_index,
    slot_index,
    norm_gain,
    router_weight,
    gate_weight,
    up_weight,
    down_weight,
    final_gain,
    head_weight,
):
    expert_devices = lax.axis_size("expert")
    model_devices = lax.axis_size("mp")
    local_tokens, local_features = tokens.shape
    expert_count = router_weight.shape[0]
    capacity = 3 * local_tokens // expert_count
    model_width = local_features * expert_devices * model_devices
    tokens_float = tokens.astype(jnp.float32)
    gained = tokens_float * norm_gain[None, :]
    router_float = router_weight.astype(jnp.float32)
    square_part = jnp.sum(tokens_float * tokens_float, axis=1)
    square_sum = lax.psum(square_part, ("expert", "mp"))
    inverse = lax.rsqrt(square_sum / model_width + epsilon)
    normed = gained * inverse[:, None]
    router_logits = lax.psum(
        jnp.dot(normed, router_float.T, precision=lax.Precision.HIGHEST), ("expert", "mp")
    )
    normed_rows = normed.astype(jnp.bfloat16)
    router_logsum = jax.nn.logsumexp(router_logits, axis=1)
    picked = jnp.take_along_axis(router_logits, expert_index, axis=1)
    gate_weights = jax.nn.softmax(picked, axis=1)
    flat_index = expert_index * capacity + slot_index
    every_slot = jnp.arange(expert_count * capacity, dtype=jnp.int32)
    chooser = jnp.any(flat_index[None, :, :] == every_slot[:, None, None], axis=2).astype(
        jnp.bfloat16
    )
    local_slots = jnp.dot(chooser, normed_rows, preferred_element_type=jnp.float32).astype(
        jnp.bfloat16
    )
    local_slots = local_slots.reshape(expert_count, capacity, 1, 1, local_features)
    arrived = lax.all_to_all(local_slots, "expert", split_axis=0, concat_axis=2, tiled=True)
    assembled = lax.all_gather(arrived, "mp", axis=3, tiled=True)
    own_slots = assembled.reshape(capacity, model_width)
    gate_matrix = gate_weight[0]
    up_matrix = up_weight[0]
    down_matrix = down_weight[0]
    row_piece = lax.all_gather(own_slots, "dp", axis=0, tiled=True)
    gate_value = lax.dot_general(
        row_piece, gate_matrix, (((1,), (1,)), ((), ())), preferred_element_type=jnp.float32
    )
    up_value = lax.dot_general(
        row_piece, up_matrix, (((1,), (1,)), ((), ())), preferred_element_type=jnp.float32
    )
    hidden = (jax.nn.silu(gate_value) * up_value).astype(jnp.bfloat16)
    row_sums = lax.psum_scatter(
        jnp.dot(hidden, down_matrix, preferred_element_type=jnp.float32).astype(jnp.bfloat16),
        "dp",
        scatter_dimension=0,
        tiled=True,
    ).astype(jnp.float32)
    summed = lax.psum_scatter(
        row_sums.reshape(capacity, expert_devices, model_devices, local_features).astype(
            jnp.bfloat16
        ),
        "mp",
        scatter_dimension=2,
        tiled=True,
    ).astype(jnp.float32)
    expert_out = summed.reshape(1, capacity, expert_devices, local_features).astype(jnp.bfloat16)
    returned = lax.all_to_all(expert_out, "expert", split_axis=2, concat_axis=0, tiled=True)
    flat_out = returned.reshape(expert_count * capacity, local_features)
    picked_rows = jnp.take(flat_out, flat_index, axis=0)
    combined = jnp.sum(gate_weights[:, :, None] * picked_rows.astype(jnp.float32), axis=1)
    layer_out = (tokens_float + combined).astype(jnp.bfloat16)
    head_rows = lax.all_gather(layer_out, ("expert", "mp"), axis=1, tiled=True)
    head_float = head_rows.astype(jnp.float32)
    head_scale = lax.rsqrt(jnp.mean(head_float * head_float, axis=1) + epsilon)
    head_in = (head_float * head_scale[:, None] * final_gain[None, :]).astype(jnp.bfloat16)
    logits = lax.dot_general(
        head_in, head_weight, (((1,), (1,)), ((), ())), preferred_element_type=jnp.float32
    )
    vocab_max = jnp.max(logits, axis=1)
    vocab_total = jnp.sum(jnp.exp(logits - vocab_max[:, None]), axis=1)
    merged_max, merged_total = merged((vocab_max, vocab_total), ("expert", "mp"), merge_softmax)
    head_logsum = merged_max + jnp.log(merged_total)
    router_square, head_square = lax.psum(
        (jnp.sum(router_logsum * router_logsum), jnp.sum(head_logsum * head_logsum)), "dp"
    )
    token_total = local_tokens * lax.axis_size("dp")
    return (layer_out, head_logsum, router_square / token_total, head_square / token_total)


def solution(mesh):
    in_specs = (
        P("dp", ("expert", "mp")),
        P("dp", None),
        P("dp", None),
        P(("expert", "mp")),
        P(None, ("expert", "mp")),
        P("expert", ("dp", "mp"), None),
        P("expert", ("dp", "mp"), None),
        P("expert", ("dp", "mp"), None),
        P(),
        P(("expert", "mp"), None),
    )
    out_specs = (P("dp", ("expert", "mp")), P("dp"), P(), P())
    return jax.shard_map(body, mesh=mesh, in_specs=in_specs, out_specs=out_specs, check_vma=False)
```

profile of v0, /device:TPU:0, one launch (start us, length us, event | category | flops | bytes accessed | tf_op | source)
XLA Modules:
  0.0 365.9 jit_solution(3463087684671705557)
XLA Ops:
  7.2 0.7 compare_and_fusion
  8.2 1.0 fusion.29
  9.2 35.0 %psum.28 = f32[256]{0:T(256)S(1)} all-reduce(f32[256]{0:T(256)S(1)} %fusion.29), channel_id=1, replica_groups=mesh['dp'=2,'expert'=4,'mp'=4] {'expert','mp'}, use_global_device_ids=true, to_apply=%region_1.0 | all-reduce | flops 256 | bytes 2048 | tf_op jit(solution)/shard_map/psum | solution.py:47
  44.2 1.3 convolution_convert_fusion
  45.5 11.9 %all_to_all.33 = bf16[4,192,1,1,256]{4,1,3,2,0:T(8,128)(2,1)} all-to-all(bf16[4,192,1,1,256]{4,1,3,2,0:T(8,128)(2,1)S(1)} %bitcast.72), channel_id=1, replica_groups=mesh['dp'=2,'expert'=4,'mp'=4] {'expert'}, dimensions={0} | all-to-all | bytes 786432 | tf_op jit(solution)/shard_map/all_to_all | solution.py:66
  57.5 18.3 %all-gather.13.cloned.1.call-done = bf16[1,192,4,4,1,256]{5,1,4,2,0,3:T(8,128)(2,1)} async-done(((bf16[1,192,4,1,1,256]{5,1,4,2,0,3:T(8,128)(2,1)}), bf16[1,192,4,4,1,256]{5,1,4,2,0,3:T(8,128)(2,1)}) %all-gather.13.cloned.1.call-update) | async-done | bytes 1572880 | tf_op jit(solution)/shard_map/all_gather | solution.py:67
  75.8 2.6 copy.71
  78.5 2.4 reshape.84
  80.9 45.0 %all-gather.9.cloned.1.call-done = bf16[384,4096]{1,0:T(8,128)(2,1)} async-done(((bf16[192,4096]{1,0:T(8,128)(2,1)}), bf16[384,4096]{1,0:T(8,128)(2,1)}) %all-gather.9.cloned.1.call-update) | async-done | bytes 3145744 | tf_op jit(solution)/shard_map/all_gather | solution.py:72
  125.9 8.7 %fusion.4 = f32[384,896]{1,0:T(8,128)} fusion(bf16[384,4096]{1,0:T(8,128)(2,1)} %all-gather.9.cloned.1.call-done, bf16[1,896,4096]{2,1,0:T(8,128)(2,1)} %param.17), kind=kOutput, calls=%fused_computation.9 | convolution fusion | flops 2818572288 | bytes 11862016 | tf_op jit(solution)/shard_map/dot_general | solution.py:73
  134.6 14.0 %fusion.6 = bf16[384,4096]{1,0:T(8,128)(2,1)} fusion(bf16[1,896,4096]{2,1,0:T(8,128)(2,1)} %param.19, bf16[384,4096]{1,0:T(8,128)(2,1)S(1)} %copy-done.3, bf16[1,896,4096]{2,1,0:T(8,128)(2,1)} %param.18, f32[384,896]{1,0:T(8,128)} %fusion.4), kind=kOutput, calls=%fused_computation.11 | convolution fusion | flops 5640781824 | bytes 22347776 | tf_op jit(solution)/shard_map/dot_general | solution.py:81
  148.9 43.4 %reduce-scatter.5.cloned.1.call-done = bf16[192,4096]{1,0:T(8,128)(2,1)} async-done(((bf16[384,4096]{1,0:T(8,128)(2,1)}), bf16[192,4096]{1,0:T(8,128)(2,1)}) %reduce-scatter.5.cloned.1.call-update) | async-done | bytes 1572880 | tf_op jit(solution)/shard_map/reduce_scatter | solution.py:80
  192.3 2.9 convert_element_type.52
  195.2 1.7 copy.72
  198.0 33.6 %psum.29 = f32[256,4]{0,1:T(4,128)S(1)} all-reduce(f32[256,4]{0,1:T(4,128)S(1)} %fusion.27), channel_id=1, replica_groups=mesh['dp'=2,'expert'=4,'mp'=4] {'expert','mp'}, use_global_device_ids=true, to_apply=%region_2.0 | all-reduce | flops 1024 | bytes 8192 | tf_op jit(solution)/shard_map/psum | solution.py:50
  231.6 4.8 %gather_fusion.1 = f32[512]{0:T(512)S(1)} fusion(f32[256,4]{0,1:T(4,128)S(1)} %psum.29, s32[512]{0:T(512)S(1)} %reshape.94), kind=kCustom, calls=%fused_computation.1 | custom fusion | bytes 8192 | tf_op jit(solution)/shard_map/jit(take_along_axis)/gather | solution.py:55
  237.3 3.1 all-reduce.4.cloned.1.call-done
  240.4 2.4 dynamic-slice_bitcast_fusion
  242.8 4.6 %all-to-all-start.1 = ((bf16[1,192,4,256]{3,1,0,2:T(8,128)(2,1)}), bf16[1,192,4,256]{3,1,0,2:T(8,128)(2,1)S(1)}, u32[]{:S(2)}, u32[]{:S(2)}) async-start(bf16[1,192,4,256]{3,1,0,2:T(8,128)(2,1)} %dynamic-slice_bitcast_fusion), calls=%async_computation.2 | async-start | bytes 786432 | tf_op jit(solution)/shard_map/all_to_all | solution.py:95
  247.6 11.3 %all-to-all-done.1 = bf16[1,192,4,256]{3,1,0,2:T(8,128)(2,1)S(1)} async-done(((bf16[1,192,4,256]{3,1,0,2:T(8,128)(2,1)}), bf16[1,192,4,256]{3,1,0,2:T(8,128)(2,1)S(1)}, u32[]{:S(2)}, u32[]{:S(2)}) %all-to-all-start.1) | async-done | bytes 393248 | tf_op jit(solution)/shard_map/all_to_all | solution.py:95
  258.9 1.9 gather_fusion
  261.0 1.5 multiply_reduce_fusion
  262.5 0.7 fusion.30
  263.2 0.6 multiply_reduce_fusion.2
  263.8 38.7 %all-gather.11.cloned.1.call-done = bf16[256,4096]{1,0:T(8,128)(2,1)} async-done(((bf16[256,256]{1,0:T(8,128)(2,1)}), bf16[256,4096]{1,0:T(8,128)(2,1)}) %all-gather.11.cloned.1.call-update) | async-done | bytes 2097168 | tf_op jit(solution)/shard_map/all_gather | solution.py:100
  302.6 2.1 fusion.9
  304.7 6.5 %fusion.40 = (f32[256]{0:T(256)S(1)}, f32[256,1024]{1,0:T(8,128)S(1)}) fusion(bf16[1024,4096]{1,0:T(8,128)(2,1)} %param.21, bf16[256,4096]{1,0:T(8,128)(2,1)} %all-gather.11.cloned.1.call-done, f32[4096]{0:T(1024)S(1)} %copy-done.4, f32[256]{0:T(256)S(1)} %add_rsqrt_fusion), kind=kOutput, calls=%fused_computation.62 | convolution fusion | flops 2151939840 | bytes 11552768 | tf_op jit(solution)/shard_map/dot_general | solution.py:104
  311.2 19.4 %all-gather.3 = f32[16,1,256]{2,1,0:T(1,128)S(1)} all-gather(f32[1,1,256]{2,1,0:T(1,128)S(1)} %bitcast.79), channel_id=3, replica_groups=mesh['dp'=2,'expert'=4,'mp'=4] {'expert','mp'}, dimensions={0}, use_global_device_ids=true | all-gather | bytes 17408 | tf_op jit(solution)/shard_map/all_gather | solution.py:10
  330.8 17.5 %all-gather.4 = f32[16,1,256]{2,1,0:T(1,128)S(1)} all-gather(f32[1,1,256]{2,1,0:T(1,128)S(1)} %bitcast.80), channel_id=4, replica_groups=mesh['dp'=2,'expert'=4,'mp'=4] {'expert','mp'}, dimensions={0}, use_global_device_ids=true | all-gather | bytes 17408 | tf_op jit(solution)/shard_map/all_gather | solution.py:10
  348.3 0.8 while.12
  349.1 1.2 multiply_reduce_fusion.1
  350.3 5.5 %all-reduce.1 = (f32[]{:T(128)}, f32[]{:T(128)}) all-reduce(f32[]{:T(128)} %multiply_reduce_fusion.2, f32[]{:T(128)} %get-tuple-element.48), channel_id=1, replica_groups=mesh['dp'=2,'expert'=4,'mp'=4] {'dp'}, use_global_device_ids=true, to_apply=%region_17.18 | all-reduce | flops 2 | bytes 16 | tf_op jit(solution)/shard_map/psum | solution.py:111
  (84 shorter events, 3.7 us)
Async XLA Ops:
  7.2 190.6 %copy-start = (bf16[4,256]{1,0:T(4,128)(2,1)S(1)}, bf16[4,256]{1,0:T(4,128)(2,1)}, u32[]{:S(2)}) copy-start(bf16[4,256]{1,0:T(4,128)(2,1)} %param.16) | copy-start | bytes 6148
  7.2 68.6 %all-gather.13.cloned.1.call-start = ((), (), s32[]{:S(2)}) async-start(), calls=%async_computation.6 | async-start | bytes 1966080 | tf_op jit(solution)/shard_map/all_gather | solution.py:67
  57.4 68.5 %all-gather.9.cloned.1.call-start = ((), (), s32[]{:S(2)}) async-start(), calls=%async_computation.3 | async-start | bytes 4718592 | tf_op jit(solution)/shard_map/all_gather | solution.py:72
  80.8 111.4 %reduce-scatter.5.cloned.1.call-start = ((), (), s32[]{:S(2)}) async-start(), calls=%async_computation.4 | async-start | bytes 4718592 | tf_op jit(solution)/shard_map/reduce_scatter | solution.py:80
  125.9 8.7 %copy-start.3 = (bf16[384,4096]{1,0:T(8,128)(2,1)S(1)}, bf16[384,4096]{1,0:T(8,128)(2,1)}, u32[]{:S(2)}) copy-start(bf16[384,4096]{1,0:T(8,128)(2,1)} %all-gather.9.cloned.1.call-done) | copy-start | bytes 9437188
  148.7 91.7 %all-reduce.4.cloned.1.call-start = ((), (), s32[]{:S(2)}) async-start(), calls=%async_computation.7 | async-start | bytes 3145728
  195.1 2.3 copy-start.2
  195.2 2.6 copy-start.1
  195.2 2.6 copy-start.5
  231.6 5.1 %copy-start.6 = (u32[32]{0:T(128)S(1)}, u32[32]{0:T(128)}, u32[]{:S(2)}) copy-start(u32[32]{0:T(128)} %constant.81) | copy-start | bytes 388
  242.8 16.1 %all-to-all-start.1 = ((bf16[1,192,4,256]{3,1,0,2:T(8,128)(2,1)}), bf16[1,192,4,256]{3,1,0,2:T(8,128)(2,1)S(1)}, u32[]{:S(2)}, u32[]{:S(2)}) async-start(bf16[1,192,4,256]{3,1,0,2:T(8,128)(2,1)} %dynamic-slice_bitcast_fusion), calls=%async_computation.2 | async-start | bytes 786432 | tf_op jit(solution)/shard_map/all_to_all | solution.py:95
  247.3 55.2 %all-gather.11.cloned.1.call-start = ((), (), s32[]{:S(2)}) async-start(), calls=%async_computation.5 | async-start | bytes 2228224 | tf_op jit(solution)/shard_map/all_gather | solution.py:100
  258.9 45.8 %copy-start.4 = (f32[4096]{0:T(1024)S(1)}, f32[4096]{0:T(1024)}, u32[]{:S(2)}) copy-start(f32[4096]{0:T(1024)} %param.20) | copy-start | bytes 49156
Sparse Core Ops, SparseCore 0:
  57.6 18.2 all-gather.12
  81.0 44.8 all-gather.8
  148.8 43.4 reduce-scatter.4
  197.0 43.2 all-reduce.3
  263.3 39.2 all-gather.10
where the time goes:
time: 366 us
  waiting for transfers between devices  160 us (44%)
  blocking collectives  123 us (34%)
  matrix products  30.7 us (8%)
  local copies, waits for them, and re-layouts  20.8 us (6%)
  between operations  17.6 us (5%)
  other arithmetic  8.81 us (2%)
  starting transfers between devices  4.9 us (1%)
    all_gather x1, waiting for transfers between devices, body(): row_piece = lax.all_gather(own_slots, 'dp', axis=0, tiled=True)  45 us
    reduce_scatter x1, waiting for transfers between devices, body(): lax.psum_scatter(jnp.dot(hidden, down_matrix, preferred_element_type=jnp....  43.4 us
    all_gather x1, waiting for transfers between devices, body(): head_rows = lax.all_gather(layer_out, ('expert', 'mp'), axis=1, tiled=True)  38.7 us
    all_gather x2, blocking collectives, merged(): pieces = jax.tree.map(lambda part: lax.all_gather(part, axis), value)  36.8 us
    psum x1, blocking collectives, body(): square_sum = lax.psum(square_part, ('expert', 'mp'))  35 us
    psum x1, blocking collectives, body(): lax.psum(jnp.dot(normed, router_float.T, precision=lax.Precision.HIGHEST)...  33.6 us
    all_gather x1, waiting for transfers between devices, body(): assembled = lax.all_gather(arrived, 'mp', axis=3, tiled=True)  18.3 us
    dot_general x1, matrix products, body(): jnp.dot(hidden, down_matrix, preferred_element_type=jnp.float32)  14 us
  transfers between devices with their start and end apart: 6, of which 6 were waited for; matrix products, arithmetic and copies ran while one was open for 2% of the time, Pallas kernels for 0%

commit v1 on v0

v1 whole, which is shorter than its diff:
```python
import functools
import jax
import jax.numpy as jnp
from jax import lax
from jax.experimental import pallas as pl
from jax.experimental.pallas import tpu as pltpu
from jax.sharding import PartitionSpec as P

epsilon = 1e-05
MESH = pl.DeviceIdType.MESH
F32 = jnp.float32
BF16 = jnp.bfloat16
NT = (((1,), (1,)), ((), ()))
VMEM_LIMIT = 64 * 1024 * 1024 - 65536


def remote(src, dst, send_sem, recv_sem, device):
    return pltpu.make_async_remote_copy(
        src_ref=src,
        dst_ref=dst,
        send_sem=send_sem,
        recv_sem=recv_sem,
        device_id=device,
        device_id_type=MESH,
    )


def greet(devices):
    barrier = pltpu.get_barrier_semaphore()
    for device in devices:
        pl.semaphore_signal(barrier, inc=1, device_id=device, device_id_type=MESH)
    pl.semaphore_wait(barrier, len(devices))


def arrival_order(count):
    order = [0]
    for step in range(1, count // 2 + 1):
        order.append(step)
        if count - step != step:
            order.append(count - step)
    return order[:count]


class Place:
    def __init__(self, sizes):
        self.X, self.Z, self.MP = sizes
        self.C = 2 if self.MP % 2 == 0 else 1
        self.Y = self.MP // self.C
        self.x = lax.axis_index("dp")
        self.z = lax.axis_index("expert")
        self.m = lax.axis_index("mp")
        self.y = self.m // self.C
        self.c = lax.rem(self.m, self.C)
        self.linear = self.z * self.MP + self.m
        self.swap = self.X == self.Y
        self.first = (1 - self.c) if self.swap else 1
        self.S1, self.S2 = self.X, self.Y

    def plane_peer(self, j):
        other = lax.rem(self.linear + j, self.Z * self.MP)
        return (self.x, other // self.MP, lax.rem(other, self.MP))

    def z_peer(self, j):
        return (self.x, lax.rem(self.z + j, self.Z), self.m)

    def x_peer(self, j):
        return (lax.rem(self.x + j, self.X), self.z, self.m)

    def y_peer(self, j):
        return (self.x, self.z, lax.rem(self.y + j, self.Y) * self.C + self.c)

    def c_peer(self, j):
        return (self.x, self.z, self.y * self.C + lax.rem(self.c + j, self.C))

    def moved(self, first, d1, d2):
        if not self.swap:
            return lax.rem(self.x + d1, self.X), lax.rem(self.y + d2, self.Y)
        return (
            lax.rem(self.x + first * d1 + (1 - first) * d2, self.X),
            lax.rem(self.y + (1 - first) * d1 + first * d2, self.Y),
        )

    def peer(self, d1, d2):
        x, y = self.moved(self.first, d1, d2)
        return (x, self.z, y * self.C + self.c)


def layer_kernel(
    sizes,
    experts,
    top,
    capacity,
    tokens_ref,
    index_ref,
    gain_ref,
    router_ref,
    gate_ref,
    up_ref,
    down_ref,
    out_ref,
    logsum_ref,
    stat,
    stats,
    turned,
    slots,
    rows,
    wgu,
    wd,
    hidden,
    part,
    got_c,
    sum_c,
    got_p,
    sum_p,
    got_q,
    final,
    back,
    stat_send,
    stat_recv,
    own_sem,
    z_send,
    z_recv,
    g_send,
    g_recv,
    w_sem,
    c_send,
    c_recv,
    p_send,
    p_recv,
    q_send,
    q_recv,
    r_send,
    r_recv,
):
    place = Place(sizes)
    X, Z, MP, Y, C = place.X, place.Z, place.MP, place.Y, place.C
    S1, S2 = place.S1, place.S2
    x, z, m, c = place.x, place.z, place.m, place.c
    N = Z * MP
    count, lf = tokens_ref.shape
    width = N * lf
    tiles, _, tile, _ = wgu.shape
    padded = router_ref.shape[0]

    weight_copies = []
    for t in range(tiles):
        for which, source in ((0, gate_ref), (1, up_ref)):
            weight_copies.append(
                pltpu.make_async_copy(
                    source.at[pl.ds(t * tile, tile), :], wgu.at[t, which], w_sem.at[2 * t + which]
                )
            )
    down_copy = pltpu.make_async_copy(down_ref, wd, w_sem.at[2 * tiles])
    for copy in weight_copies:
        copy.start()
    down_copy.start()

    tok = tokens_ref[...].astype(F32)
    gained = tok * gain_ref[...]
    high = lax.Precision.HIGHEST
    stat[0:padded] = lax.dot_general(
        router_ref[...], gained, NT, precision=high, preferred_element_type=F32
    )
    stat[padded : padded + 8] = lax.dot_general(
        jnp.ones((8, lf), F32), tok * tok, NT, precision=high, preferred_element_type=F32
    )
    stats[pl.ds(place.linear, 1)] = stat[...][None]

    greet(
        [place.plane_peer(j) for j in range(1, N)] + [place.x_peer(j) for j in range(1, X)]
    )

    sends = []
    for j in range(1, N):
        copy = remote(
            stat, stats.at[place.linear], stat_send.at[j], stat_recv.at[j], place.plane_peer(j)
        )
        copy.start()
        sends.append(copy)
    for copy in sends:
        copy.wait_recv()

    total = stats[0]
    for j in range(1, N):
        total = total + stats[j]
    inverse = lax.rsqrt(total[padded : padded + 1] / width + epsilon)
    logits = total[0:experts] * inverse
    peak = jnp.max(logits, axis=0, keepdims=True)
    logsum_ref[...] = peak + jnp.log(jnp.sum(jnp.exp(logits - peak), axis=0, keepdims=True))
    index = index_ref[...]
    numbers = lax.broadcasted_iota(jnp.int32, (experts, count), 0)
    picked = [
        jnp.sum(jnp.where(numbers == index[k : k + 1], logits, 0.0), axis=0, keepdims=True)
        for k in range(top)
    ]
    top_peak = functools.reduce(jnp.maximum, picked)
    raised = [jnp.exp(value - top_peak) for value in picked]
    weight_sum = functools.reduce(jnp.add, raised)
    turned[...] = jnp.zeros_like(turned)
    turned[0:1] = inverse
    for k in range(top):
        turned[1 + k : 2 + k] = raised[k] / weight_sum
        turned[1 + top + k : 2 + top + k] = index[top + k : top + k + 1].astype(F32)
    columns = jnp.transpose(turned[...])

    normed = (gained * columns[:, 0:1]).astype(BF16)
    for e in range(experts):
        every = lax.broadcasted_iota(jnp.int32, (capacity, count), 0) + e * capacity
        chosen = every == index[top : top + 1]
        for k in range(1, top):
            chosen = jnp.logical_or(chosen, every == index[top + k : top + k + 1])
        slots[e] = jnp.dot(
            jnp.where(chosen, 1.0, 0.0).astype(BF16), normed, preferred_element_type=F32
        ).astype(BF16)

    def block(sx, sz, sm):
        return rows.at[
            pl.ds(pl.multiple_of(sx * capacity, capacity), capacity),
            pl.ds(pl.multiple_of((sz * MP + sm) * lf, lf), lf),
        ]

    order = arrival_order(Z)
    own = pltpu.make_async_copy(slots.at[z], block(x, z, m), own_sem.at[0])
    own.start()
    z_copies = {}
    for j in order[1:]:
        copy = remote(
            slots.at[lax.rem(z + j, Z)], block(x, z, m), z_send.at[j], z_recv.at[j], place.z_peer(j)
        )
        copy.start()
        sends.append(copy)
        z_copies[j] = copy

    def sem_at(k, d1, d2, dc):
        return ((k * S1 + d1) * S2 + d2) * C + dc

    def source(k, d1, d2, dc):
        sc = lax.rem(c + C - dc, C)
        first = (1 - sc) if place.swap else 1
        sx, sy = place.moved(first, lax.rem(S1 - d1, S1), lax.rem(S2 - d2, S2))
        return block(sx, lax.rem(z + Z - k, Z), sy * C + sc)

    def forward(k, d1, d2, axis):
        held = source(k, d1, d2, 0)
        if axis == 0:
            targets = [((d, d2, 0), place.peer(d, 0)) for d in range(1, S1)]
        elif axis == 1:
            targets = [((d1, d, 0), place.peer(0, d)) for d in range(1, S2)]
        else:
            targets = [((d1, d2, d), place.c_peer(d)) for d in range(1, C)]
        for spot, device in targets:
            at = sem_at(k, *spot)
            copy = remote(held, held, g_send.at[at], g_recv.at[at], device)
            copy.start()
            sends.append(copy)

    def wait_for(k, d1, d2, dc):
        held = source(k, d1, d2, dc)
        at = sem_at(k, d1, d2, dc)
        remote(held, held, g_send.at[at], g_recv.at[at], place.z_peer(1)).wait_recv()

    def hop_own(k):
        if k == 0:
            own.wait()
        else:
            z_copies[k].wait_recv()
        forward(k, 0, 0, 0)
        forward(k, 0, 0, 1)
        forward(k, 0, 0, 2)

    def hop_first(k):
        for d in range(1, S1):
            wait_for(k, d, 0, 0)
            forward(k, d, 0, 1)
            forward(k, d, 0, 2)
        for d in range(1, S2):
            wait_for(k, 0, d, 0)
            forward(k, 0, d, 2)

    def hop_second(k):
        for d1 in range(1, S1):
            for d2 in range(1, S2):
                wait_for(k, d1, d2, 0)
                forward(k, d1, d2, 2)

    for step in range(Z + 2):
        if step < Z:
            hop_own(order[step])
        if 0 <= step - 1 < Z:
            hop_first(order[step - 1])
        if 0 <= step - 2 < Z:
            hop_second(order[step - 2])
    for k in order:
        for d1 in range(S1):
            for d2 in range(S2):
                for dc in range(1, C):
                    wait_for(k, d1, d2, dc)

    for copy in weight_copies:
        copy.wait()

    if tile % 128 == 0:

        def expert_tile(t, carry):
            both = lax.dot_general(
                rows[...], wgu[t].reshape(2 * tile, width), NT, preferred_element_type=F32
            )
            gate_value, up_value = both[:, :tile], both[:, tile:]
            value = gate_value / (1.0 + jnp.exp(-gate_value)) * up_value
            hidden[:, pl.ds(pl.multiple_of(t * tile, tile), tile)] = value.astype(BF16)
            return carry

        lax.fori_loop(0, tiles, expert_tile, 0)
    else:
        for t in range(tiles):
            gate_value = lax.dot_general(rows[...], wgu[t, 0], NT, preferred_element_type=F32)
            up_value = lax.dot_general(rows[...], wgu[t, 1], NT, preferred_element_type=F32)
            value = gate_value / (1.0 + jnp.exp(-gate_value)) * up_value
            hidden[:, t * tile : (t + 1) * tile] = value.astype(BF16)

    down_copy.wait()
    back_order = order[1:] + [0]
    c_copies, p_copies, q_copies, r_copies = {}, {}, {}, {}

    def down_block(k, ty, dc):
        tz = lax.rem(z + k, Z)
        tm = ty * C + lax.rem(c + dc, C)
        at = pl.multiple_of((tz * MP + tm) * lf, lf)
        part[k, ty, dc] = jnp.dot(
            hidden[...], wd[:, pl.ds(at, lf)], preferred_element_type=F32
        ).astype(BF16)

    def stage_down(k):
        for dc in list(range(1, C)) + [0]:

            def one(ty, carry, dc=dc):
                down_block(k, ty, dc)
                return carry

            lax.fori_loop(0, Y, one, 0)
            if dc:
                copy = remote(
                    part.at[k, :, dc],
                    got_c.at[k, dc],
                    c_send.at[k * C + dc],
                    c_recv.at[k * C + dc],
                    place.c_peer(dc),
                )
                copy.start()
                sends.append(copy)
                c_copies[k, dc] = copy

    def stage_c(k):
        value = part[k, :, 0].astype(F32)
        for dc in range(1, C):
            c_copies[k, dc].wait_recv()
            value = value + got_c[k, dc].astype(F32)
        sum_c[k] = value.astype(BF16)
        for i in range(1, S2):
            for d1 in range(S1):
                tx, ty = place.moved(place.first, d1, i)
                at = (k * S2 + i) * S1 + d1
                copy = remote(
                    sum_c.at[k, ty, pl.ds(pl.multiple_of(tx * capacity, capacity), capacity)],
                    got_p.at[k, i, d1],
                    p_send.at[at],
                    p_recv.at[at],
                    place.peer(0, i),
                )
                copy.start()
                sends.append(copy)
                p_copies[k, i, d1] = copy

    def stage_p(k):
        for d1 in list(range(1, S1)) + [0]:
            tx, ty = place.moved(place.first, d1, 0)
            value = sum_c[
                k, ty, pl.ds(pl.multiple_of(tx * capacity, capacity), capacity)
            ].astype(F32)
            for i in range(1, S2):
                p_copies[k, i, d1].wait_recv()
                value = value + got_p[k, i, d1].astype(F32)
            sum_p[k, d1] = value.astype(BF16)
            if d1:
                at = k * S1 + d1
                copy = remote(
                    sum_p.at[k, d1], got_q.at[k, d1], q_send.at[at], q_recv.at[at], place.peer(d1, 0)
                )
                copy.start()
                sends.append(copy)
                q_copies[k, d1] = copy

    def stage_q(k):
        value = sum_p[k, 0].astype(F32)
        for d1 in range(1, S1):
            q_copies[k, d1].wait_recv()
            value = value + got_q[k, d1].astype(F32)
        if k == 0:
            back[pl.ds(z, 1)] = value.astype(BF16)[None]
        else:
            final[k] = value.astype(BF16)
            copy = remote(final.at[k], back.at[z], r_send.at[k], r_recv.at[k], place.z_peer(k))
            copy.start()
            sends.append(copy)
            r_copies[k] = copy

    for step in range(Z + 3):
        if step < Z:
            stage_down(back_order[step])
        if 0 <= step - 1 < Z:
            stage_c(back_order[step - 1])
        if 0 <= step - 2 < Z:
            stage_p(back_order[step - 2])
        if 0 <= step - 3 < Z:
            stage_q(back_order[step - 3])
    for k in order[1:]:
        r_copies[k].wait_recv()

    returned = back[...].reshape(experts * capacity, lf)
    every = lax.broadcasted_iota(jnp.int32, (count, experts * capacity), 1).astype(F32)
    combined = jnp.zeros((count, lf), F32)
    for k in range(top):
        chosen = jnp.where(every == columns[:, 1 + top + k : 2 + top + k], 1.0, 0.0).astype(BF16)
        combined = combined + columns[:, 1 + k : 2 + k] * jnp.dot(
            chosen, returned, preferred_element_type=F32
        )
    out_ref[...] = (tokens_ref[...].astype(F32) + combined).astype(BF16)
    for copy in sends:
        copy.wait_send()


def head_kernel(
    sizes,
    layer_ref,
    router_logsum_ref,
    gain_ref,
    weight_ref,
    logsum_ref,
    penalty_ref,
    full,
    weight,
    head_in,
    logits,
    pair,
    pairs,
    square,
    squares,
    w_sem,
    z_send,
    z_recv,
    g_send,
    g_recv,
    pair_send,
    pair_recv,
    square_send,
    square_recv,
):
    place = Place(sizes)
    X, Z, MP, Y, C = place.X, place.Z, place.MP, place.Y, place.C
    x, z, m, y, c = place.x, place.z, place.m, place.y, place.c
    N = Z * MP
    count, lf = layer_ref.shape
    width = N * lf
    vocabulary = weight_ref.shape[0]

    weight_copy = pltpu.make_async_copy(weight_ref, weight, w_sem.at[0])
    weight_copy.start()
    greet(
        [place.plane_peer(j) for j in range(1, N)] + [place.x_peer(j) for j in range(1, X)]
    )

    def block(sz, sm):
        return full.at[:, pl.ds(pl.multiple_of((sz * MP + sm) * lf, lf), lf)]

    order = arrival_order(Z)
    sends = []
    z_copies = {}
    own = pltpu.make_async_copy(layer_ref, block(z, m), w_sem.at[1])
    own.start()
    for j in order[1:]:
        copy = remote(layer_ref, block(z, m), z_send.at[j], z_recv.at[j], place.z_peer(j))
        copy.start()
        sends.append(copy)
        z_copies[j] = copy

    def sem_at(k, dy, dc):
        return (k * Y + dy) * C + dc

    def source(k, dy, dc):
        sy = lax.rem(y + Y - dy, Y)
        return block(lax.rem(z + Z - k, Z), sy * C + lax.rem(c + C - dc, C))

    def send(k, dy, dc, held, device):
        at = sem_at(k, dy, dc)
        copy = remote(held, held, g_send.at[at], g_recv.at[at], device)
        copy.start()
        sends.append(copy)

    def wait_for(k, dy, dc):
        held = source(k, dy, dc)
        at = sem_at(k, dy, dc)
        remote(held, held, g_send.at[at], g_recv.at[at], place.z_peer(1)).wait_recv()

    def hop_own(k):
        if k == 0:
            own.wait()
        else:
            z_copies[k].wait_recv()
        held = source(k, 0, 0)
        for d in range(1, Y):
            send(k, d, 0, held, place.y_peer(d))
        for d in range(1, C):
            send(k, 0, d, held, place.c_peer(d))

    def hop_y(k):
        for dy in range(1, Y):
            wait_for(k, dy, 0)
            for d in range(1, C):
                send(k, dy, d, source(k, dy, 0), place.c_peer(d))

    for step in range(Z + 1):
        if step < Z:
            hop_own(order[step])
        if step >= 1:
            hop_y(order[step - 1])
    for k in order:
        for dy in range(Y):
            for dc in range(1, C):
                wait_for(k, dy, dc)

    chunk = 32 if count % 32 == 0 else count

    def norm_rows(r, carry):
        at = pl.ds(pl.multiple_of(r * chunk, chunk), chunk)
        value = full[at, :].astype(F32)
        scale = lax.rsqrt(jnp.mean(value * value, axis=1, keepdims=True) + epsilon)
        head_in[at, :] = (value * scale * gain_ref[...]).astype(BF16)
        return carry

    lax.fori_loop(0, count // chunk, norm_rows, 0)
    weight_copy.wait()
    tile = 256 if vocabulary % 256 == 0 else vocabulary

    def vocab_tile(t, peak):
        at = pl.ds(pl.multiple_of(t * tile, tile), tile)
        value = lax.dot_general(weight[at, :], head_in[...], NT, preferred_element_type=F32)
        logits[at, :] = value
        return jnp.maximum(peak, jnp.max(value, axis=0, keepdims=True))

    start = jnp.full((1, count), -jnp.inf, F32)
    peak = lax.fori_loop(0, vocabulary // tile, vocab_tile, start)
    pair[0:1] = peak
    pair[1:2] = jnp.sum(jnp.exp(logits[...] - peak), axis=0, keepdims=True)
    pair[2:8] = jnp.zeros((6, count), F32)
    pairs[pl.ds(place.linear, 1)] = pair[...][None]
    pair_copies = []
    for j in range(1, N):
        copy = remote(
            pair, pairs.at[place.linear], pair_send.at[j], pair_recv.at[j], place.plane_peer(j)
        )
        copy.start()
        pair_copies.append(copy)
    for copy in pair_copies:
        copy.wait_recv()
    everything = pairs[...]
    peaks, totals = everything[:, 0, :], everything[:, 1, :]
    merged = jnp.max(peaks, axis=0, keepdims=True)
    logsum = merged + jnp.log(jnp.sum(totals * jnp.exp(peaks - merged), axis=0, keepdims=True))
    logsum_ref[...] = logsum
    router_logsum = router_logsum_ref[...]
    square[...] = jnp.zeros_like(square)
    square[0:1] = jnp.broadcast_to(
        jnp.sum(router_logsum * router_logsum, axis=1, keepdims=True), (1, square.shape[1])
    )
    square[1:2] = jnp.broadcast_to(
        jnp.sum(logsum * logsum, axis=1, keepdims=True), (1, square.shape[1])
    )
    squares[pl.ds(x, 1)] = square[...][None]
    square_copies = []
    for j in range(1, X):
        copy = remote(
            square, squares.at[x], square_send.at[j], square_recv.at[j], place.x_peer(j)
        )
        copy.start()
        square_copies.append(copy)
    for copy in square_copies:
        copy.wait_recv()
    total = squares[0]
    for j in range(1, X):
        total = total + squares[j]
    penalty_ref[...] = total / (count * X)
    for copy in sends + pair_copies + square_copies:
        copy.wait_send()


def body(
    sizes,
    tokens,
    expert_index,
    slot_index,
    norm_gain,
    router_weight,
    gate_weight,
    up_weight,
    down_weight,
    final_gain,
    head_weight,
):
    X, Z, MP = sizes
    C = 2 if MP % 2 == 0 else 1
    Y = MP // C
    N = Z * MP
    count, lf = tokens.shape
    top = expert_index.shape[1]
    experts = router_weight.shape[0]
    capacity = 3 * count // experts
    _, ff, width = gate_weight.shape
    vocabulary = head_weight.shape[0]
    padded = -(-experts // 8) * 8
    flat = expert_index * capacity + slot_index
    index = jnp.concatenate([expert_index, flat], axis=1).T
    router = jnp.pad(router_weight.astype(F32), ((0, padded - experts), (0, 0)))
    tile = 128 if ff % 128 == 0 else ff
    vmem = pl.BlockSpec(memory_space=pltpu.VMEM)
    anywhere = pl.BlockSpec(memory_space=pl.ANY)
    dma = pltpu.SemaphoreType.DMA
    params = functools.partial(
        pltpu.CompilerParams, has_side_effects=True, vmem_limit_bytes=VMEM_LIMIT
    )
    layer_out, router_logsum = pl.pallas_call(
        functools.partial(layer_kernel, sizes, experts, top, capacity),
        out_shape=(
            jax.ShapeDtypeStruct((count, lf), BF16),
            jax.ShapeDtypeStruct((1, count), F32),
        ),
        in_specs=[vmem] * 4 + [anywhere] * 3,
        out_specs=(vmem, vmem),
        scratch_shapes=[
            pltpu.VMEM((padded + 8, count), F32),
            pltpu.VMEM((N, padded + 8, count), F32),
            pltpu.VMEM((128, count), F32),
            pltpu.VMEM((experts, capacity, lf), BF16),
            pltpu.VMEM((X * capacity, width), BF16),
            pltpu.VMEM((ff // tile, 2, tile, width), BF16),
            pltpu.VMEM((ff, width), BF16),
            pltpu.VMEM((X * capacity, ff), BF16),
            pltpu.VMEM((Z, Y, C, X * capacity, lf), BF16),
            pltpu.VMEM((Z, C, Y, X * capacity, lf), BF16),
            pltpu.VMEM((Z, Y, X * capacity, lf), BF16),
            pltpu.VMEM((Z, Y, X, capacity, lf), BF16),
            pltpu.VMEM((Z, X, capacity, lf), BF16),
            pltpu.VMEM((Z, X, capacity, lf), BF16),
            pltpu.VMEM((Z, capacity, lf), BF16),
            pltpu.VMEM((Z, capacity, lf), BF16),
            dma((N,)),
            dma((N,)),
            dma((1,)),
            dma((Z,)),
            dma((Z,)),
            dma((Z * X * Y * C,)),
            dma((Z * X * Y * C,)),
            dma((2 * (ff // tile) + 1,)),
            dma((Z * C,)),
            dma((Z * C,)),
            dma((Z * X * Y,)),
            dma((Z * X * Y,)),
            dma((Z * X,)),
            dma((Z * X,)),
            dma((Z,)),
            dma((Z,)),
        ],
        compiler_params=params(collective_id=0),
        name="layer",
    )(
        tokens,
        index,
        norm_gain[None, :],
        router,
        gate_weight[0],
        up_weight[0],
        down_weight[0],
    )
    logsum, penalty = pl.pallas_call(
        functools.partial(head_kernel, sizes),
        out_shape=(
            jax.ShapeDtypeStruct((1, count), F32),
            jax.ShapeDtypeStruct((8, 128), F32),
        ),
        in_specs=[vmem] * 3 + [anywhere],
        out_specs=(vmem, vmem),
        scratch_shapes=[
            pltpu.VMEM((count, width), BF16),
            pltpu.VMEM((vocabulary, width), BF16),
            pltpu.VMEM((count, width), BF16),
            pltpu.VMEM((vocabulary, count), F32),
            pltpu.VMEM((8, count), F32),
            pltpu.VMEM((N, 8, count), F32),
            pltpu.VMEM((8, 128), F32),
            pltpu.VMEM((X, 8, 128), F32),
            dma((2,)),
            dma((Z,)),
            dma((Z,)),
            dma((N,)),
            dma((N,)),
            dma((N,)),
            dma((N,)),
            dma((X,)),
            dma((X,)),
        ],
        compiler_params=params(collective_id=1),
        name="head",
    )(layer_out, router_logsum, final_gain[None, :], head_weight)
    return (layer_out, logsum[0], penalty[0, 0], penalty[1, 0])


def solution(mesh):
    in_specs = (
        P("dp", ("expert", "mp")),
        P("dp", None),
        P("dp", None),
        P(("expert", "mp")),
        P(None, ("expert", "mp")),
        P("expert", ("dp", "mp"), None),
        P("expert", ("dp", "mp"), None),
        P("expert", ("dp", "mp"), None),
        P(),
        P(("expert", "mp"), None),
    )
    out_specs = (P("dp", ("expert", "mp")), P("dp"), P(), P())
    sizes = (mesh.shape["dp"], mesh.shape["expert"], mesh.shape["mp"])
    return jax.shard_map(
        functools.partial(body, sizes),
        mesh=mesh,
        in_specs=in_specs,
        out_specs=out_specs,
        check_vma=False,
    )
```

time: 366 us -> 112 us (0.31)
  waiting for transfers between devices: 160 us -> 0 us
  blocking collectives: 123 us -> 0 us
  Pallas kernels: 0 us -> 104 us
  matrix products: 30.7 us -> 0 us
  between operations: 17.6 us -> 0.65 us
  local copies, waits for them, and re-layouts: 20.8 us -> 4.02 us
  other arithmetic: 8.81 us -> 3.26 us
  starting transfers between devices: 4.9 us -> 0 us
    pallas_call x0 -> x2, Pallas kernels: none -> 104 us  [the longest x1 70.3 us: body(): pl.pallas_call(functools.partial(layer_kernel, sizes, experts, top, capac...]
    all_gather x3 -> x0, waiting for transfers between devices: 102 us -> none  [the longest x1 45 us: body(): row_piece = lax.all_gather(own_slots, 'dp', axis=0, tiled=True)]
    psum x3 -> x0, blocking collectives: 74.1 us -> none  [the longest x1 35 us: body(): square_sum = lax.psum(square_part, ('expert', 'mp'))]
    reduce_scatter x1 -> x0, waiting for transfers between devices: 43.4 us -> none  [body(): lax.psum_scatter(jnp.dot(hidden, down_matrix, preferred_element_type=jnp....]
    all_gather x2 -> x0, blocking collectives: 36.8 us -> none  [merged(): pieces = jax.tree.map(lambda part: lax.all_gather(part, axis), value)]
    dot_general x5 -> x0, matrix products: 30.7 us -> none  [the longest x1 14 us: body(): jnp.dot(hidden, down_matrix, preferred_element_type=jnp.float32)]
    all_to_all x1 -> x0, blocking collectives: 11.9 us -> none  [body(): lax.all_to_all(local_slots, 'expert', split_axis=0, concat_axis=2, tiled=...]
    all_to_all x1 -> x0, waiting for transfers between devices: 11.3 us -> none  [body(): lax.all_to_all(expert_out, 'expert', split_axis=2, concat_axis=0, tiled=T...]
  transfers between devices with their start and end apart: 6 -> 0, of which waited for: 6 -> 0; matrix products, arithmetic and copies ran while one was open for 2% -> 0% of each run, Pallas kernels for 0% -> 0%
where the time goes in v1:
time: 112 us
  Pallas kernels  104 us (93%)
  local copies, waits for them, and re-layouts  4.02 us (4%)
  other arithmetic  3.26 us (3%)
    pallas_call x1, Pallas kernels, body(): pl.pallas_call(functools.partial(layer_kernel, sizes, experts, top, capac...  70.3 us
    pallas_call x1, Pallas kernels, body(): pl.pallas_call(functools.partial(head_kernel, sizes), out_shape=(jax.Shap...  33.5 us
    unnamed x2, local copies, waits for them, and re-layouts  2.75 us

profile of v1, /device:TPU:0, one launch (start us, length us, event | category | flops | bytes accessed | tf_op | source)
XLA Modules:
  0.0 111.7 jit_solution(16666874888710786914)
XLA Ops:
  0.6 1.3 %pad_convert_fusion.router_ref = f32[8,256]{1,0:T(8,128)} fusion(bf16[4,256]{1,0:T(4,128)(2,1)} %param.14), kind=kLoop, calls=%fused_computation.1 | loop fusion | flops 2048 | bytes 10240 | tf_op jit(solution)/shard_map/jit(_pad)/pad | solution.py:622
  1.9 0.7 multiply_add_fusion
  2.6 1.3 %add_bitcast_fusion.index_ref = s32[4,256]{1,0:T(4,128)} fusion(s32[256,2]{0,1:T(2,128)S(1)} %multiply_add_fusion, s32[256,2]{0,1:T(2,128)} %param.11), kind=kLoop, calls=%fused_computation | loop fusion | flops 1024 | bytes 8192 | tf_op jit(solution)/shard_map/transpose | solution.py:621
  3.9 70.3 %layer.1 = (bf16[256,256]{1,0:T(8,128)(2,1)}, f32[1,256]{1,0:T(1,128)}) custom-call(bf16[256,256]{1,0:T(8,128)(2,1)} %tokens_ref.1, s32[4,256]{1,0:T(4,128)} %add_bitcast_fusion.index_ref, f32[1,256]{1,0:T(1,128)} %bitcast.14, f32[8,256]{1,0:T(8,128)} %pad_convert_fusion.router_ref, bf16[896,4096]{1,0:T(8,128)(2,1)} %bitcast.10, bf16[896,4096]{1,0:T(8,128)(2,1)} %bitcast.11, ...), custom_call_target="tpu_custom_call" | custom-call | tf_op jit(solution)/shard_map/layer/pallas_call | solution.py:630
  74.2 33.5 %head.1 = (f32[1,256]{1,0:T(1,128)}, f32[8,128]{1,0:T(8,128)}) custom-call(bf16[256,256]{1,0:T(8,128)(2,1)} %get-tuple-element.18.layer_ref, f32[1,256]{1,0:T(1,128)} %get-tuple-element.9.router_logsum_ref, f32[1,4096]{1,0:T(1,128)} %bitcast.13, bf16[1024,4096]{1,0:T(8,128)(2,1)} %weight_ref.1), custom_call_target="tpu_custom_call" | custom-call | tf_op jit(solution)/shard_map/head/pallas_call | solution.py:683
  107.7 1.3 %fusion = (f32[1,1]{1,0:T(1,128)}, f32[1,1]{1,0:T(1,128)}) fusion(f32[8,128]{1,0:T(8,128)} %get-tuple-element.11), kind=kLoop, calls=%fused_computation.3 | loop fusion | bytes 16 | tf_op jit(solution)/shard_map/slice | solution.py:713
  109.0 1.6 %copy.16 = bf16[256,256]{1,0:T(8,128)(2,1)} copy(bf16[256,256]{1,0:T(8,128)(2,1)} %get-tuple-element.18.layer_ref) | data formatting | bytes 262144
  110.6 1.2 %copy.17 = f32[256]{0:T(256)} copy(f32[256]{0:T(256)} %bitcast.15) | data formatting | bytes 2048

commit v2 on v1

--- a/solution.py
+++ b/solution.py
@@ -85,20 +85,25 @@
         return (x, self.z, y * self.C + self.c)
 
 
-def layer_kernel(
+def layer_part(
     sizes,
+    sends,
+    head_weight_copy,
     experts,
     top,
     capacity,
     tokens_ref,
-    index_ref,
+    expert_ref,
+    slot_ref,
     gain_ref,
     router_ref,
     gate_ref,
     up_ref,
     down_ref,
     out_ref,
-    logsum_ref,
+    router,
+    flipped,
+    acc,
     stat,
     stats,
     turned,
@@ -140,7 +145,6 @@
     count, lf = tokens_ref.shape
     width = N * lf
     tiles, _, tile, _ = wgu.shape
-    padded = router_ref.shape[0]
 
     weight_copies = []
     for t in range(tiles):
@@ -154,40 +158,47 @@
     for copy in weight_copies:
         copy.start()
     down_copy.start()
+    head_weight_copy.start()
 
     tok = tokens_ref[...].astype(F32)
     gained = tok * gain_ref[...]
     high = lax.Precision.HIGHEST
-    stat[0:padded] = lax.dot_general(
-        router_ref[...], gained, NT, precision=high, preferred_element_type=F32
-    )
-    stat[padded : padded + 8] = lax.dot_general(
+    router[...] = jnp.zeros_like(router)
+    router[0:experts] = router_ref[...].astype(F32)
+    router_part = lax.dot_general(
+        router[...], gained, NT, precision=high, preferred_element_type=F32
+    )
+    square_part = lax.dot_general(
         jnp.ones((8, lf), F32), tok * tok, NT, precision=high, preferred_element_type=F32
-    )
+    )[0:1]
+    line = lax.broadcasted_iota(jnp.int32, stat.shape, 0)
+    stat[...] = jnp.where(line == experts, square_part, router_part)
     stats[pl.ds(place.linear, 1)] = stat[...][None]
 
     greet(
         [place.plane_peer(j) for j in range(1, N)] + [place.x_peer(j) for j in range(1, X)]
     )
 
-    sends = []
     for j in range(1, N):
         copy = remote(
             stat, stats.at[place.linear], stat_send.at[j], stat_recv.at[j], place.plane_peer(j)
         )
         copy.start()
         sends.append(copy)
+    flipped[...] = jnp.zeros_like(flipped)
+    flipped[:, 0:top] = expert_ref[...].astype(F32)
+    flipped[:, top : 2 * top] = (expert_ref[...] * capacity + slot_ref[...]).astype(F32)
+    index = jnp.transpose(flipped[...])[0 : 2 * top].astype(jnp.int32)
     for copy in sends:
         copy.wait_recv()
 
     total = stats[0]
     for j in range(1, N):
         total = total + stats[j]
-    inverse = lax.rsqrt(total[padded : padded + 1] / width + epsilon)
+    inverse = lax.rsqrt(total[experts : experts + 1] / width + epsilon)
     logits = total[0:experts] * inverse
     peak = jnp.max(logits, axis=0, keepdims=True)
-    logsum_ref[...] = peak + jnp.log(jnp.sum(jnp.exp(logits - peak), axis=0, keepdims=True))
-    index = index_ref[...]
+    router_logsum = peak + jnp.log(jnp.sum(jnp.exp(logits - peak), axis=0, keepdims=True))
     numbers = lax.broadcasted_iota(jnp.int32, (experts, count), 0)
     picked = [
         jnp.sum(jnp.where(numbers == index[k : k + 1], logits, 0.0), axis=0, keepdims=True)
@@ -283,40 +294,62 @@
                 wait_for(k, d1, d2, 0)
                 forward(k, d1, d2, 2)
 
-    for step in range(Z + 2):
+    def arrive(k):
+        for d1 in range(S1):
+            for d2 in range(S2):
+                for dc in range(1, C):
+                    wait_for(k, d1, d2, dc)
+
+    chunk = MP * lf
+
+    def multiply(k, begin, end):
+        at = pl.ds(pl.multiple_of(lax.rem(z + Z - k, Z) * chunk, chunk), chunk)
+
+        def expert_tile(t, carry):
+            held = rows[:, at]
+            if tile % 128 == 0:
+                both = lax.dot_general(
+                    held,
+                    wgu[t, :, :, at].reshape(2 * tile, chunk),
+                    NT,
+                    preferred_element_type=F32,
+                )
+                gate_value, up_value = both[:, :tile], both[:, tile:]
+            else:
+                gate_value = lax.dot_general(held, wgu[t, 0, :, at], NT, preferred_element_type=F32)
+                up_value = lax.dot_general(held, wgu[t, 1, :, at], NT, preferred_element_type=F32)
+            if not begin:
+                gate_value = gate_value + acc[t, 0]
+                up_value = up_value + acc[t, 1]
+            if end:
+                value = gate_value / (1.0 + jnp.exp(-gate_value)) * up_value
+                if tiles == 1:
+                    hidden[...] = value.astype(BF16)
+                else:
+                    hidden[:, pl.ds(pl.multiple_of(t * tile, tile), tile)] = value.astype(BF16)
+            else:
+                acc[t, 0] = gate_value
+                acc[t, 1] = up_value
+            return carry
+
+        if tiles == 1:
+            expert_tile(0, 0)
+        else:
+            lax.fori_loop(0, tiles, expert_tile, 0)
+
+    for step in range(Z + 3):
         if step < Z:
             hop_own(order[step])
         if 0 <= step - 1 < Z:
             hop_first(order[step - 1])
         if 0 <= step - 2 < Z:
             hop_second(order[step - 2])
-    for k in order:
-        for d1 in range(S1):
-            for d2 in range(S2):
-                for dc in range(1, C):
-                    wait_for(k, d1, d2, dc)
-
-    for copy in weight_copies:
-        copy.wait()
-
-    if tile % 128 == 0:
-
-        def expert_tile(t, carry):
-            both = lax.dot_general(
-                rows[...], wgu[t].reshape(2 * tile, width), NT, preferred_element_type=F32
-            )
-            gate_value, up_value = both[:, :tile], both[:, tile:]
-            value = gate_value / (1.0 + jnp.exp(-gate_value)) * up_value
-            hidden[:, pl.ds(pl.multiple_of(t * tile, tile), tile)] = value.astype(BF16)
-            return carry
-
-        lax.fori_loop(0, tiles, expert_tile, 0)
-    else:
-        for t in range(tiles):
-            gate_value = lax.dot_general(rows[...], wgu[t, 0], NT, preferred_element_type=F32)
-            up_value = lax.dot_general(rows[...], wgu[t, 1], NT, preferred_element_type=F32)
-            value = gate_value / (1.0 + jnp.exp(-gate_value)) * up_value
-            hidden[:, t * tile : (t + 1) * tile] = value.astype(BF16)
+        if 0 <= step - 3 < Z:
+            if step == 3:
+                for copy in weight_copies:
+                    copy.wait()
+            arrive(order[step - 3])
+            multiply(order[step - 3], step == 3, step == Z + 2)
 
     down_copy.wait()
     back_order = order[1:] + [0]
@@ -425,27 +458,26 @@
             chosen, returned, preferred_element_type=F32
         )
     out_ref[...] = (tokens_ref[...].astype(F32) + combined).astype(BF16)
-    for copy in sends:
-        copy.wait_send()
-
-
-def head_kernel(
+    return router_logsum
+
+
+def head_part(
     sizes,
+    sends,
+    weight_copy,
+    router_logsum,
     layer_ref,
-    router_logsum_ref,
     gain_ref,
-    weight_ref,
     logsum_ref,
     penalty_ref,
     full,
     weight,
-    head_in,
     logits,
     pair,
     pairs,
     square,
     squares,
-    w_sem,
+    layer_sem,
     z_send,
     z_recv,
     g_send,
@@ -461,21 +493,14 @@
     N = Z * MP
     count, lf = layer_ref.shape
     width = N * lf
-    vocabulary = weight_ref.shape[0]
-
-    weight_copy = pltpu.make_async_copy(weight_ref, weight, w_sem.at[0])
-    weight_copy.start()
-    greet(
-        [place.plane_peer(j) for j in range(1, N)] + [place.x_peer(j) for j in range(1, X)]
-    )
+    vocabulary = weight.shape[0]
 
     def block(sz, sm):
         return full.at[:, pl.ds(pl.multiple_of((sz * MP + sm) * lf, lf), lf)]
 
     order = arrival_order(Z)
-    sends = []
     z_copies = {}
-    own = pltpu.make_async_copy(layer_ref, block(z, m), w_sem.at[1])
+    own = pltpu.make_async_copy(layer_ref, block(z, m), layer_sem.at[0])
     own.start()
     for j in order[1:]:
         copy = remote(layer_ref, block(z, m), z_send.at[j], z_recv.at[j], place.z_peer(j))
@@ -518,40 +543,53 @@
             for d in range(1, C):
                 send(k, dy, d, source(k, dy, 0), place.c_peer(d))
 
-    for step in range(Z + 1):
-        if step < Z:
-            hop_own(order[step])
-        if step >= 1:
-            hop_y(order[step - 1])
-    for k in order:
+    def arrive(k):
         for dy in range(Y):
             for dc in range(1, C):
                 wait_for(k, dy, dc)
 
-    chunk = 32 if count % 32 == 0 else count
-
-    def norm_rows(r, carry):
-        at = pl.ds(pl.multiple_of(r * chunk, chunk), chunk)
-        value = full[at, :].astype(F32)
-        scale = lax.rsqrt(jnp.mean(value * value, axis=1, keepdims=True) + epsilon)
-        head_in[at, :] = (value * scale * gain_ref[...]).astype(BF16)
-        return carry
-
-    lax.fori_loop(0, count // chunk, norm_rows, 0)
-    weight_copy.wait()
     tile = 256 if vocabulary % 256 == 0 else vocabulary
-
-    def vocab_tile(t, peak):
-        at = pl.ds(pl.multiple_of(t * tile, tile), tile)
-        value = lax.dot_general(weight[at, :], head_in[...], NT, preferred_element_type=F32)
-        logits[at, :] = value
-        return jnp.maximum(peak, jnp.max(value, axis=0, keepdims=True))
-
-    start = jnp.full((1, count), -jnp.inf, F32)
-    peak = lax.fori_loop(0, vocabulary // tile, vocab_tile, start)
-    pair[0:1] = peak
-    pair[1:2] = jnp.sum(jnp.exp(logits[...] - peak), axis=0, keepdims=True)
-    pair[2:8] = jnp.zeros((6, count), F32)
+    chunk = MP * lf
+
+    def multiply(k, begin):
+        at = pl.ds(pl.multiple_of(lax.rem(z + Z - k, Z) * chunk, chunk), chunk)
+        value = full[:, at].astype(F32)
+        held = (value * gain_ref[:, at]).astype(BF16)
+
+        def vocab_tile(t, carry):
+            spot = pl.ds(pl.multiple_of(t * tile, tile), tile)
+            product = lax.dot_general(weight[spot, at], held, NT, preferred_element_type=F32)
+            if not begin:
+                product = product + logits[spot, :]
+            logits[spot, :] = product
+            return carry
+
+        lax.fori_loop(0, vocabulary // tile, vocab_tile, 0)
+        return jnp.sum(value * value, axis=1, keepdims=True)
+
+    square_sum = jnp.zeros((count, 1), F32)
+    for step in range(Z + 2):
+        if step < Z:
+            hop_own(order[step])
+        if 0 <= step - 1 < Z:
+            hop_y(order[step - 1])
+        if 0 <= step - 2 < Z:
+            if step == 2:
+                weight_copy.wait()
+            arrive(order[step - 2])
+            square_sum = square_sum + multiply(order[step - 2], step == 2)
+
+    scale = lax.rsqrt(
+        jnp.transpose(jnp.broadcast_to(square_sum, (count, 128)))[0:1] / width + epsilon
+    )
+    scaled = logits[...] * scale
+    peak = jnp.max(scaled, axis=0, keepdims=True)
+    total = jnp.sum(jnp.exp(scaled - peak), axis=0, keepdims=True)
+    groups = count // 128
+    pair[...] = jnp.zeros_like(pair)
+    for g in range(groups):
+        pair[g : g + 1] = peak[:, g * 128 : (g + 1) * 128]
+        pair[groups + g : groups + g + 1] = total[:, g * 128 : (g + 1) * 128]
     pairs[pl.ds(place.linear, 1)] = pair[...][None]
     pair_copies = []
     for j in range(1, N):
@@ -563,17 +601,17 @@
     for copy in pair_copies:
         copy.wait_recv()
     everything = pairs[...]
-    peaks, totals = everything[:, 0, :], everything[:, 1, :]
-    merged = jnp.max(peaks, axis=0, keepdims=True)
-    logsum = merged + jnp.log(jnp.sum(totals * jnp.exp(peaks - merged), axis=0, keepdims=True))
+    peaks, totals = everything[:, 0:groups, :], everything[:, groups : 2 * groups, :]
+    merged = jnp.max(peaks, axis=0)
+    logsum = merged + jnp.log(jnp.sum(totals * jnp.exp(peaks - merged[None]), axis=0))
     logsum_ref[...] = logsum
-    router_logsum = router_logsum_ref[...]
     square[...] = jnp.zeros_like(square)
     square[0:1] = jnp.broadcast_to(
         jnp.sum(router_logsum * router_logsum, axis=1, keepdims=True), (1, square.shape[1])
     )
     square[1:2] = jnp.broadcast_to(
-        jnp.sum(logsum * logsum, axis=1, keepdims=True), (1, square.shape[1])
+        jnp.sum(jnp.sum(logsum * logsum, axis=1, keepdims=True), axis=0, keepdims=True),
+        (1, square.shape[1]),
     )
     squares[pl.ds(x, 1)] = square[...][None]
     square_copies = []
@@ -591,6 +629,28 @@
     penalty_ref[...] = total / (count * X)
     for copy in sends + pair_copies + square_copies:
         copy.wait_send()
+
+
+def kernel(sizes, experts, top, capacity, split, *refs):
+    layer_in, (head_gain, head_weight) = refs[:8], refs[8:10]
+    out_ref, logsum_ref, penalty_ref = refs[10:13]
+    layer_scratch, head_scratch = refs[13 : 13 + split], refs[13 + split : -1]
+    head_weight_copy = pltpu.make_async_copy(head_weight, head_scratch[1], refs[-1].at[0])
+    sends = []
+    router_logsum = layer_part(
+        sizes, sends, head_weight_copy, experts, top, capacity, *layer_in, out_ref, *layer_scratch
+    )
+    head_part(
+        sizes,
+        sends,
+        head_weight_copy,
+        router_logsum,
+        out_ref,
+        head_gain,
+        logsum_ref,
+        penalty_ref,
+        *head_scratch,
+    )
 
 
 def body(
@@ -616,28 +676,19 @@
     capacity = 3 * count // experts
     _, ff, width = gate_weight.shape
     vocabulary = head_weight.shape[0]
-    padded = -(-experts // 8) * 8
-    flat = expert_index * capacity + slot_index
-    index = jnp.concatenate([expert_index, flat], axis=1).T
-    router = jnp.pad(router_weight.astype(F32), ((0, padded - experts), (0, 0)))
+    padded = -(-(experts + 1) // 8) * 8
+    groups = count // 128
+    pair_rows = -(-2 * groups // 8) * 8
     tile = 128 if ff % 128 == 0 else ff
     vmem = pl.BlockSpec(memory_space=pltpu.VMEM)
     anywhere = pl.BlockSpec(memory_space=pl.ANY)
     dma = pltpu.SemaphoreType.DMA
-    params = functools.partial(
-        pltpu.CompilerParams, has_side_effects=True, vmem_limit_bytes=VMEM_LIMIT
-    )
-    layer_out, router_logsum = pl.pallas_call(
-        functools.partial(layer_kernel, sizes, experts, top, capacity),
-        out_shape=(
-            jax.ShapeDtypeStruct((count, lf), BF16),
-            jax.ShapeDtypeStruct((1, count), F32),
-        ),
-        in_specs=[vmem] * 4 + [anywhere] * 3,
-        out_specs=(vmem, vmem),
-        scratch_shapes=[
-            pltpu.VMEM((padded + 8, count), F32),
-            pltpu.VMEM((N, padded + 8, count), F32),
+    layer_scratch = [
+            pltpu.VMEM((padded, lf), F32),
+            pltpu.VMEM((count, 128), F32),
+            pltpu.VMEM((ff // tile, 2, X * capacity, tile), F32),
+            pltpu.VMEM((padded, count), F32),
+            pltpu.VMEM((N, padded, count), F32),
             pltpu.VMEM((128, count), F32),
             pltpu.VMEM((experts, capacity, lf), BF16),
             pltpu.VMEM((X * capacity, width), BF16),
@@ -668,36 +719,16 @@
             dma((Z * X,)),
             dma((Z,)),
             dma((Z,)),
-        ],
-        compiler_params=params(collective_id=0),
-        name="layer",
-    )(
-        tokens,
-        index,
-        norm_gain[None, :],
-        router,
-        gate_weight[0],
-        up_weight[0],
-        down_weight[0],
-    )
-    logsum, penalty = pl.pallas_call(
-        functools.partial(head_kernel, sizes),
-        out_shape=(
-            jax.ShapeDtypeStruct((1, count), F32),
-            jax.ShapeDtypeStruct((8, 128), F32),
-        ),
-        in_specs=[vmem] * 3 + [anywhere],
-        out_specs=(vmem, vmem),
-        scratch_shapes=[
+    ]
+    head_scratch = [
             pltpu.VMEM((count, width), BF16),
             pltpu.VMEM((vocabulary, width), BF16),
-            pltpu.VMEM((count, width), BF16),
             pltpu.VMEM((vocabulary, count), F32),
-            pltpu.VMEM((8, count), F32),
-            pltpu.VMEM((N, 8, count), F32),
+            pltpu.VMEM((pair_rows, 128), F32),
+            pltpu.VMEM((N, pair_rows, 128), F32),
             pltpu.VMEM((8, 128), F32),
             pltpu.VMEM((X, 8, 128), F32),
-            dma((2,)),
+            dma((1,)),
             dma((Z,)),
             dma((Z,)),
             dma((N,)),
@@ -706,11 +737,34 @@
             dma((N,)),
             dma((X,)),
             dma((X,)),
-        ],
-        compiler_params=params(collective_id=1),
-        name="head",
-    )(layer_out, router_logsum, final_gain[None, :], head_weight)
-    return (layer_out, logsum[0], penalty[0, 0], penalty[1, 0])
+    ]
+    layer_out, logsum, penalty = pl.pallas_call(
+        functools.partial(kernel, sizes, experts, top, capacity, len(layer_scratch)),
+        out_shape=(
+            jax.ShapeDtypeStruct((count, lf), BF16),
+            jax.ShapeDtypeStruct((groups, 128), F32),
+            jax.ShapeDtypeStruct((8, 128), F32),
+        ),
+        in_specs=[vmem] * 5 + [anywhere] * 3 + [vmem, anywhere],
+        out_specs=(vmem, vmem, vmem),
+        scratch_shapes=layer_scratch + head_scratch + [dma((1,))],
+        compiler_params=pltpu.CompilerParams(
+            has_side_effects=True, vmem_limit_bytes=VMEM_LIMIT, collective_id=0
+        ),
+        name="scoring",
+    )(
+        tokens,
+        expert_index,
+        slot_index,
+        norm_gain[None, :],
+        router_weight,
+        gate_weight[0],
+        up_weight[0],
+        down_weight[0],
+        final_gain[None, :],
+        head_weight,
+    )
+    return (layer_out, logsum.reshape(count), penalty[0, 0], penalty[1, 0])
 
 
 def solution(mesh):

time: 112 us -> 107 us (0.955)
  Pallas kernels: 104 us -> 98.7 us
  other arithmetic: 3.26 us -> 0 us
  local copies, waits for them, and re-layouts: 4.02 us -> 7.01 us
    pallas_call x2 -> x1, Pallas kernels: 104 us -> 98.7 us  [body(): pl.pallas_call(functools.partial(kernel, sizes, experts, top, capacity, l...]
    unnamed x2 -> x4, local copies, waits for them, and re-layouts: 2.75 us -> 5.74 us
    pad x1 -> x0, other arithmetic: 1.28 us -> none  [body(): router = jnp.pad(router_weight.astype(F32), ((0, padded - experts), (0, 0)))]
    transpose x1 -> x0, other arithmetic: 1.28 us -> none  [body(): index = jnp.concatenate([expert_index, flat], axis=1).T]
where the time goes in v2:
time: 107 us; the launch traced here: 106 us
  Pallas kernels  98.7 us (92%)
  local copies, waits for them, and re-layouts  7.01 us (7%)
    pallas_call x1, Pallas kernels, body(): pl.pallas_call(functools.partial(kernel, sizes, experts, top, capacity, l...  98.7 us
    unnamed x4, local copies, waits for them, and re-layouts  5.74 us

profile of v2, /device:TPU:0, one launch (start us, length us, event | category | flops | bytes accessed | tf_op | source)
XLA Modules:
  0.0 106.3 jit_solution(14294438276883398077)
XLA Ops:
  0.6 1.5 %copy.14.refs_1_ = s32[256,2]{1,0:T(8,128)} copy(s32[256,2]{0,1:T(2,128)} %param.11) | data formatting | bytes 4096 | tf_op args[1]
  2.1 1.5 %copy.15.refs_2_ = s32[256,2]{1,0:T(8,128)} copy(s32[256,2]{0,1:T(2,128)} %param.12) | data formatting | bytes 4096 | tf_op args[2]
  3.6 98.7 %scoring.1 = (bf16[256,256]{1,0:T(8,128)(2,1)}, f32[2,128]{1,0:T(2,128)}, f32[8,128]{1,0:T(8,128)}) custom-call(bf16[256,256]{1,0:T(8,128)(2,1)} %refs_0_.1, s32[256,2]{1,0:T(8,128)} %copy.14.refs_1_, s32[256,2]{1,0:T(8,128)} %copy.15.refs_2_, f32[1,256]{1,0:T(1,128)} %bitcast.12, bf16[4,256]{1,0:T(4,128)(2,1)} %refs_4_.1, bf16[896,4096]{1,0:T(8,128)(2,1)} %bitcast.8, ...), custom_call_target="tpu_custom_call" | custom-call | tf_op jit(solution)/shard_map/scoring/pallas_call | solution.py:741
  102.3 1.3 %fusion = (f32[1,1]{1,0:T(1,128)}, f32[1,1]{1,0:T(1,128)}) fusion(f32[8,128]{1,0:T(8,128)} %get-tuple-element.9), kind=kLoop, calls=%fused_computation | loop fusion | bytes 16 | tf_op jit(solution)/shard_map/slice | solution.py:767
  103.5 1.6 %copy.18 = bf16[256,256]{1,0:T(8,128)(2,1)} copy(bf16[256,256]{1,0:T(8,128)(2,1)} %get-tuple-element.16) | data formatting | bytes 262144
  105.1 1.2 %copy.19 = f32[256]{0:T(256)} copy(f32[256]{0:T(256)} %bitcast.13) | data formatting | bytes 2048
